TPU v7x, 128 devices: a whole 4x4x4 slice. The times are simulated.
128 devices in a mesh: idx: 8 (over z, y_hi), tp: 16 (over x, y_lo, core).
Axes of the slice: x: 4, y: 4 (y_hi: 2, y_lo: 2; y = y_hi * 2 + y_lo), z: 4, core: 2. Of those that a mesh axis runs over, the one named last changes fastest.
Arguments:
- activations: bfloat16 [8192, 28672], P('idx', 'tp'), may hold values from -6 to 6
- out_grads: bfloat16 [8192, 8192], P('idx', 'tp'), may hold values from -6 to 6
- proj_in: bfloat16 [28672, 64], P('tp'), may hold values from -0.03125 to 0.03125
- proj_out: bfloat16 [8192, 64], P('tp'), may hold values from -0.0625 to 0.0625
- doc_ids: int32 [8192], P('idx'), may hold values from 0 to 1023, never falling along the last dimension, each value on 1 to 32 neighbouring positions
- doc_order: int32 [1024], replicated, may hold values from 0 to 1023, each once
- inv_fisher: float32 [4096, 4096], P('tp'), may hold values from -1 to 3, as said below
- index_grads: bfloat16 [131072, 4096], P(('idx', 'tp')), may hold values from -0.0234375 to 0.0234375
Outputs:
- scores: float32 [1024, 131072], P(None, ('idx', 'tp'))
Inputs may be any that keep to these rules, and one draw needn't show every extreme that they name: `inv_fisher`: an estimate of the inverse Fisher of the projected gradients.
All inputs are finite; a program needn't handle non-finite values.
Results may differ from a plain program's by a relative error of at most 0.0029.
Values may be sent and summed in bfloat16 or wider, within the bound.
A program may use at most 128 MiB of HBM per device.

v0:
```python
import jax
import jax.numpy as jnp
from jax import lax
from jax.sharding import PartitionSpec as P


def filled_up(lines, size):
    spare = -lines.shape[0] % size
    if not spare:
        return lines
    return jnp.concatenate([lines, jnp.zeros((spare, *lines.shape[1:]), lines.dtype)])


def laid_out(blocks, dim):
    dims = list(blocks.shape[1:])
    dims[dim] *= blocks.shape[0]
    return jnp.moveaxis(blocks, 0, dim).reshape(dims)


def copy_for_each(value, axis):
    copies = jnp.broadcast_to(value, (lax.axis_size(axis), *value.shape))
    return lax.all_to_all(copies, axis, split_axis=0, concat_axis=0, tiled=True)


def collect(value, axis, dim):
    return laid_out(copy_for_each(value, axis), dim)


def cut_along(value, dim, size):
    before, after = (value.shape[:dim], value.shape[dim + 1 :])
    return jnp.moveaxis(value.reshape(*before, size, -1, *after), dim, 0)


def summed_on_arrival(value, axis, dim):
    size = lax.axis_size(axis)
    blocks = lax.all_to_all(cut_along(value, dim, size), axis, 0, 0, tiled=True)
    return jnp.sum(blocks, axis=0)


def total_of(value, axes):
    padded = filled_up(value, lax.axis_size(axes))
    whole = collect(summed_on_arrival(padded, axes, 0), axes, 0)
    return lax.slice_in_dim(whole, 0, len(value)).reshape(value.shape)


def in_one(arrays, axis):
    ends = [0]
    for a in arrays:
        ends.append(ends[-1] + a.size)
    total = total_of(jnp.concatenate([a.ravel() for a in arrays]), axis)
    return tuple((total[b:e].reshape(a.shape) for a, b, e in zip(arrays, ends, ends[1:])))


def per_device(
    activations, out_grads, proj_in, proj_out, doc_ids, doc_order, inv_fisher, index_grads
):
    part_in = jnp.dot(activations, proj_in, preferred_element_type=jnp.float32)
    part_out = jnp.dot(out_grads, proj_out, preferred_element_type=jnp.float32)
    proj_acts, proj_grads = in_one((part_in, part_out), "tp")
    rank_width = proj_acts.shape[1]
    feature_width = inv_fisher.shape[0]
    lead_count = feature_width // rank_width
    grad_slice = lax.dynamic_slice_in_dim(
        proj_grads, lax.axis_index("tp") * lead_count, lead_count, 1
    )
    token_grads = (grad_slice[:, :, None] * proj_acts[:, None, :]).reshape(
        grad_slice.shape[0], feature_width
    )
    membership = (doc_ids[:, None] == doc_order[None, :]).astype(jnp.float32)
    partial_value = lax.dot_general(
        membership,
        token_grads,
        (((0,), (0,)), ((), ())),
        precision=lax.Precision.HIGHEST,
        preferred_element_type=jnp.float32,
    )
    owned_rows = summed_on_arrival(partial_value, "idx", 0)
    shares = summed_on_arrival(
        jnp.dot(
            owned_rows,
            inv_fisher,
            precision=lax.Precision.HIGHEST,
            preferred_element_type=jnp.float32,
        ),
        "tp",
        0,
    )
    queries = shares.astype(jnp.bfloat16)
    return lax.dot_general(
        lax.all_gather(queries, ("idx", "tp"), axis=0, tiled=True),
        index_grads,
        (((1,), (1,)), ((), ())),
        preferred_element_type=jnp.float32,
    )


def solution(mesh):
    placed = (
        P("idx", "tp"),
        P("idx", "tp"),
        P("tp", None),
        P("tp", None),
        P("idx"),
        P(),
        P("tp", None),
        P(("idx", "tp"), None),
    )
    return jax.shard_map(
        per_device, mesh=mesh, in_specs=placed, out_specs=P(None, ("idx", "tp")), check_vma=False
    )
```

profile of v0, /device:TPU:1, one launch (start us, length us, event | category | flops | bytes accessed | tf_op | source)
XLA Modules:
  0.0 327.5 jit_solution(5741420817464107070)
XLA Ops:
  6.5 3.2 fusion.7
  9.8 0.2 concatenate.8
  10.0 0.4 fusion.8
  10.4 0.2 concatenate.9
  10.6 0.5 copy.16
  11.2 16.3 %all_to_all.25 = f32[16,1,8192]{2,1,0:T(1,128)S(1)} all-to-all(f32[16,1,8192]{2,1,0:T(1,128)S(1)} %copy.16), channel_id=1, replica_groups=mesh['idx'=8,'tp'=16] {'tp'}, dimensions={0} | all-to-all | bytes 1048576 | tf_op jit(solution)/shard_map/all_to_all | solution.py:36
  27.5 0.3 reduce_sum.27
  27.8 1.2 broadcast_in_dim.2
  29.0 4.6 %all-to-all-start.1 = ((f32[16,1,8192]{2,1,0:T(1,128)}), f32[16,1,8192]{2,1,0:T(1,128)S(1)}, u32[]{:S(2)}, u32[]{:S(2)}) async-start(f32[16,1,8192]{2,1,0:T(1,128)} %broadcast_in_dim.2), calls=%async_computation.1 | async-start | bytes 1048576 | tf_op jit(solution)/shard_map/all_to_all | solution.py:22
  33.7 9.7 %all-to-all-done.1 = f32[16,1,8192]{2,1,0:T(1,128)S(1)} async-done(((f32[16,1,8192]{2,1,0:T(1,128)}), f32[16,1,8192]{2,1,0:T(1,128)S(1)}, u32[]{:S(2)}, u32[]{:S(2)}) %all-to-all-start.1) | async-done | bytes 524320 | tf_op jit(solution)/shard_map/all_to_all | solution.py:22
  43.4 1.3 slice_reduce_fusion.1
  44.7 0.2 reshape.54
  44.9 0.2 constant_dynamic-slice_fusion
  45.1 0.2 copy.17
  45.3 0.2 mul.28
  45.6 0.2 copy.18
  45.8 0.1 broadcast_multiply_fusion
  45.9 2.0 fusion.2
  47.9 22.9 %all_to_all.26 = f32[8,128,256]{2,1,0:T(8,128)S(1)} all-to-all(f32[8,128,256]{2,1,0:T(8,128)S(1)} %fusion.2), channel_id=1, replica_groups=mesh['idx'=8,'tp'=16] {'idx'}, dimensions={0} | all-to-all | bytes 2097152 | tf_op jit(solution)/shard_map/all_to_all | solution.py:36
  70.9 4.5 %fusion = f32[16,8,4096]{2,1,0:T(8,128)S(1)} fusion(f32[256,4096]{1,0:T(8,128)} %param.14, f32[128,256]{1,0:T(8,128)S(1)} %reduce_sum.28), kind=kOutput, calls=%fused_computation | convolution fusion | flops 1610612736 | bytes 6422528 | tf_op jit(solution)/shard_map/dot_general | solution.py:79
  75.5 31.8 %all_to_all.27 = f32[16,8,4096]{2,1,0:T(8,128)S(1)} all-to-all(f32[16,8,4096]{2,1,0:T(8,128)S(1)} %fusion), channel_id=1, replica_groups=mesh['idx'=8,'tp'=16] {'tp'}, dimensions={0} | all-to-all | bytes 4194304 | tf_op jit(solution)/shard_map/all_to_all | solution.py:36
  107.2 0.7 reduce_sum.29
  108.0 197.7 %all-gather.2.cloned.1.call-done = bf16[1024,4096]{1,0:T(8,128)(2,1)} async-done(((bf16[8,4096]{1,0:T(8,128)(2,1)}), bf16[1024,4096]{1,0:T(8,128)(2,1)}) %all-gather.2.cloned.1.call-update) | async-done | bytes 8388624 | tf_op jit(solution)/shard_map/all_gather | solution.py:90
  305.7 15.0 %fusion.9 = f32[1024,1024]{1,0:T(8,128)} fusion(bf16[1024,4096]{1,0:T(8,128)(2,1)} %all-gather.2.cloned.1.call-done, bf16[1024,4096]{1,0:T(8,128)(2,1)} %param.15), kind=kOutput, calls=%fused_computation.14 | convolution fusion | flops 8589934592 | bytes 20971520 | tf_op jit(solution)/shard_map/dot_general | solution.py:89
  (12 shorter events, 0.2 us)
Async XLA Ops:
  6.5 3.4 %copy-start = (bf16[1024,512]{1,0:T(8,128)(2,1)S(1)}, bf16[1024,512]{1,0:T(8,128)(2,1)}, u32[]{:S(2)}) copy-start(bf16[1024,512]{1,0:T(8,128)(2,1)} %param.9) | copy-start | bytes 3145732
  6.5 3.4 %copy-start.1 = (bf16[512,64]{0,1:T(8,128)(2,1)S(1)}, bf16[512,64]{0,1:T(8,128)(2,1)}, u32[]{:S(2)}) copy-start(bf16[512,64]{0,1:T(8,128)(2,1)} %param.11) | copy-start | bytes 196612
  27.5 18.4 %copy-start.2 = (s32[1024]{0:T(1024)S(1)}, s32[1024]{0:T(1024)}, u32[]{:S(2)}) copy-start(s32[1024]{0:T(1024)} %param.13) | copy-start | bytes 12292
  27.5 18.4 %copy-start.3 = (s32[1024]{0:T(1024)S(1)}, s32[1024]{0:T(1024)}, u32[]{:S(2)}) copy-start(s32[1024]{0:T(1024)} %param.12) | copy-start | bytes 12292
  29.0 14.3 %all-to-all-start.1 = ((f32[16,1,8192]{2,1,0:T(1,128)}), f32[16,1,8192]{2,1,0:T(1,128)S(1)}, u32[]{:S(2)}, u32[]{:S(2)}) async-start(f32[16,1,8192]{2,1,0:T(1,128)} %broadcast_in_dim.2), calls=%async_computation.1 | async-start | bytes 1048576 | tf_op jit(solution)/shard_map/all_to_all | solution.py:22
  33.6 272.0 %all-gather.2.cloned.1.call-start = ((), (), s32[]{:S(2)}) async-start(), calls=%async_computation.4 | async-start | bytes 8454144 | tf_op jit(solution)/shard_map/all_gather | solution.py:90
Sparse Core Ops, SparseCore 0:
  108.1 197.4 all-gather.1
where the time goes:
time: 328 us
  waiting for transfers between devices  207 us (63%)
  blocking collectives  71 us (22%)
  matrix products  25.2 us (8%)
  between operations  13.5 us (4%)
  starting transfers between devices  4.62 us (1%)
  local copies, waits for them, and re-layouts  4.49 us (1%)
    all_gather x1, waiting for transfers between devices, per_device(): lax.all_gather(queries, ('idx', 'tp'), axis=0, tiled=True)  198 us
    all_to_all x3, blocking collectives, summed_on_arrival(): blocks = lax.all_to_all(cut_along(value, dim, size), axis, 0, 0, tiled=True)  71 us
    dot_general x1, matrix products, per_device(): lax.dot_general(lax.all_gather(queries, ('idx', 'tp'), axis=0, tiled=True...  15 us
    all_to_all x1, waiting for transfers between devices, copy_for_each(): return lax.all_to_all(copies, axis, split_axis=0, concat_axis=0, tiled=True)  9.71 us
  transfers between devices with their start and end apart: 2, of which 2 were waited for; matrix products, arithmetic and copies ran while one was open for 0% of the time, Pallas kernels for 0%

commit v1 on v0

v1 whole, which is shorter than its diff:
```python
import functools

import jax
import jax.numpy as jnp
from jax import lax
from jax.experimental import pallas as pl
from jax.experimental.pallas import tpu as pltpu
from jax.sharding import PartitionSpec as P

MESH = pl.DeviceIdType.MESH
F32, BF16 = jnp.float32, jnp.bfloat16
AXES = "xyz"
LINKS = (("x", 0), ("y", 0), ("z", 0), ("x", 1), ("y", 1), ("z", 1))
COLOURS = 6
MESSAGES = [(s, b) for s in range(1, 7) for b in range(s)]
SLOT = {m: i for i, m in enumerate(MESSAGES)}
PASSES = 12


class Place:
    def __init__(self):
        idx, tp = lax.axis_index("idx"), lax.axis_index("tp")
        self.x, self.z = tp // 4, idx // 2
        self.y = lax.rem(idx, 2) * 2 + lax.rem(tp // 2, 2)
        self.core = lax.rem(tp, 2)

    def device(self, x=None, y=None, z=None, core=None):
        x = self.x if x is None else x
        y = self.y if y is None else y
        z = self.z if z is None else z
        core = self.core if core is None else core
        return (z * 2 + y // 2, (x * 2 + lax.rem(y, 2)) * 2 + core)

    def across(self, axis, kind):
        v = getattr(self, axis)
        if kind:
            return lax.rem(v + 3 + 2 * lax.rem(v, 2), 4)
        return v + 1 - 2 * lax.rem(v, 2)

    def mate(self):
        return self.device(core=1 - self.core)

    def next_to(self, axis, kind):
        return self.device(**{axis: self.across(axis, kind)})


def order_of(colour):
    return [LINKS[(colour + s) % 6] for s in range(6)]


def turned(colour, axis):
    order = order_of(colour)
    return 1 if order.index((axis, 1)) < order.index((axis, 0)) else 0


def spot(v, turn):
    return lax.rem(v + 3 * turn, 4)


def boxes_at(colour, where):
    own = {a: spot(where[a], turned(colour, a)) for a in AXES}
    seen = dict.fromkeys(AXES, 0)

    def held(a):
        p = own[a]
        return ((p, 1), (p - lax.rem(p, 2), 2), (0, 4))[seen[a]]

    boxes = [{a: held(a) for a in AXES}]
    for axis, _ in order_of(colour):
        box = {a: held(a) for a in AXES}
        p = own[axis]
        box[axis] = (2 * (1 - p // 2), 2) if seen[axis] else (p + 1 - 2 * lax.rem(p, 2), 1)
        boxes.append(box)
        seen[axis] += 1
    return boxes


def part_of(buf, core, box):
    return buf.at[core, pl.ds(*box["z"]), pl.ds(*box["y"]), pl.ds(*box["x"])]


class Gather:
    def __init__(self, me, bufs, sems):
        self.me, self.bufs = me, bufs
        self.out_sem, self.in_sem, self.pass_out, self.pass_in = sems
        here = {a: getattr(me, a) for a in AXES}
        self.boxes = [boxes_at(k, here) for k in range(COLOURS)]
        self.theirs = []
        for k in range(COLOURS):
            per_step = []
            for axis, kind in order_of(k):
                per_step.append(boxes_at(k, {**here, axis: me.across(axis, kind)}))
            self.theirs.append(per_step)

    @staticmethod
    def semaphores():
        dma = pltpu.SemaphoreType.DMA
        return [dma((COLOURS, 21)), dma((COLOURS, 21)), dma((COLOURS, PASSES)), dma((COLOURS, PASSES))]

    def message(self, k, s, b):
        ref = part_of(self.bufs[k], self.me.core, self.boxes[k][b])
        axis, kind = order_of(k)[s - 1]
        return pltpu.make_async_remote_copy(
            src_ref=ref, dst_ref=ref,
            send_sem=self.out_sem.at[k, SLOT[s, b]], recv_sem=self.in_sem.at[k, SLOT[s, b]],
            device_id=self.me.next_to(axis, kind), device_id_type=MESH)

    def arrival(self, k, s, b):
        ref = part_of(self.bufs[k], self.me.core, self.theirs[k][s - 1][b])
        axis, kind = order_of(k)[s - 1]
        return pltpu.make_async_remote_copy(
            src_ref=ref, dst_ref=ref,
            send_sem=self.out_sem.at[k, SLOT[s, b]], recv_sem=self.in_sem.at[k, SLOT[s, b]],
            device_id=self.me.next_to(axis, kind), device_id_type=MESH)

    def pass_box(self, k, n):
        return self.boxes[k][n] if n < 6 else self.theirs[k][5][n - 6]

    def passed(self, k, n, core):
        ref = part_of(self.bufs[k], core, self.pass_box(k, n))
        return pltpu.make_async_remote_copy(
            src_ref=ref, dst_ref=ref,
            send_sem=self.pass_out.at[k, n], recv_sem=self.pass_in.at[k, n],
            device_id=self.me.mate(), device_id_type=MESH)

    def start(self):
        for s in range(1, 7):
            for k in range(COLOURS):
                self.message(k, s, 0).start()
            if s == 1:
                for k in range(COLOURS):
                    self.passed(k, 0, self.me.core).start()

    def step(self, s):
        for k in range(COLOURS):
            for b in range(s):
                self.arrival(k, s, b).wait_recv()
            for later in range(s + 1, 7):
                self.message(k, later, s).start()
            self.passed(k, s, self.me.core).start()

    def last(self, b):
        for k in range(COLOURS):
            self.arrival(k, 6, b).wait_recv()
            self.passed(k, 6 + b, self.me.core).start()

    def from_mate(self, n):
        for k in range(COLOURS):
            self.passed(k, n, 1 - self.me.core).wait_recv()

    def close(self):
        for k in range(COLOURS):
            for s, b in MESSAGES:
                self.message(k, s, b).wait_send()
            for n in range(PASSES):
                self.passed(k, n, self.me.core).wait_send()


def greet(devices):
    barrier = pltpu.get_barrier_semaphore()
    for device in devices:
        pl.semaphore_signal(barrier, inc=1, device_id=device, device_id_type=MESH)
    pl.semaphore_wait(barrier, len(devices))


Q_TILES = (3, 3, 3, 3, 2, 2)
Q_FIRST = (0, 3, 6, 9, 12, 14)


def scores_kernel(blk_ref, g_hbm, out_ref, b0, b1, b2, b3, b4, b5, g_ref, g_sem, *sems):
    me = Place()
    bufs = (b0, b1, b2, b3, b4, b5)
    load = pltpu.make_async_copy(g_hbm, g_ref, g_sem)
    load.start()
    gather = Gather(me, bufs, sems)
    for k in range(COLOURS):
        own = gather.boxes[k][0]
        bufs[k][me.core, own["z"][0], own["y"][0], own["x"][0]] = blk_ref[Q_FIRST[k]:Q_FIRST[k] + Q_TILES[k]]
    greet([me.next_to(a, t) for a, t in LINKS] + [me.mate()])
    gather.start()
    for s in range(1, 6):
        gather.step(s)
    for b in range(6):
        gather.last(b)
    for n in range(PASSES):
        gather.from_mate(n)
    load.wait()

    @pl.loop(0, 8)
    def _(chunk):
        z_low, y = chunk // 4, lax.rem(chunk, 4)
        depth = pl.multiple_of(chunk * 512, 512)
        g = g_ref[:, pl.ds(depth, 512)]
        for z_high in range(2):
            for core in range(2):
                cols = []
                for x in range(4):
                    rows = []
                    for k in range(COLOURS):
                        tile = bufs[k][core, spot(z_high * 2 + z_low, turned(k, "z")),
                                       spot(y, turned(k, "y")), (x + 3 * turned(k, "x")) % 4]
                        rows.append(tile.reshape(Q_TILES[k] * 16, 128))
                    cols.append(jnp.concatenate(rows, 0))
                lhs = jnp.concatenate(cols, 1)
                got = lax.dot_general(lhs, g, (((1,), (1,)), ((), ())), preferred_element_type=F32)
                rows = pl.ds((core * 2 + z_high) * 256, 256)

                @pl.when(chunk == 0)
                def _():
                    out_ref[rows, :] = got

                @pl.when(chunk > 0)
                def _():
                    out_ref[rows, :] += got

    gather.close()


def scores_call(block, index_grads):
    vmem = pl.BlockSpec(memory_space=pltpu.VMEM)
    return pl.pallas_call(
        scores_kernel,
        out_shape=jax.ShapeDtypeStruct((1024, 1024), F32),
        in_specs=[vmem, pl.BlockSpec(memory_space=pl.ANY)],
        out_specs=vmem,
        scratch_shapes=[pltpu.VMEM((2, 4, 4, 4, n, 16, 128), BF16) for n in Q_TILES]
        + [pltpu.VMEM((1024, 4096), BF16), pltpu.SemaphoreType.DMA] + Gather.semaphores(),
        compiler_params=pltpu.CompilerParams(collective_id=3, has_side_effects=True, vmem_limit_bytes=48 << 20),
        name="scores",
    )(block, index_grads)


T_UNITS = (3, 3, 3, 3, 2, 2)
T_FIRST = (0, 3, 6, 9, 12, 14)
OTHERS_TP = [(dx, dy) for dx in range(4) for dy in range(2)][1:]
OTHERS_IDX = [(dz, dy) for dz in range(4) for dy in range(2)][1:]
PITCH = 264


def halves(v):
    high = v.astype(BF16)
    return high, (v - high.astype(F32)).astype(BF16)


def queries_kernel(
    part_ref, f_hbm, counts_ref, out_ref,
    from_mate, mine, arrived, t0, t1, t2, t3, t4, t5, tok, fisher, their_counts, counts_sum, counts, dg, acc, lacc,
    mate_sem, rs_out, rs_in, f_out, f_in, f_pass, f_own, c_out, c_in, c_sem, *sems):
    me = Place()
    bufs = (t0, t1, t2, t3, t4, t5)
    low = lax.rem(me.y, 2)
    high = me.y // 2
    p = low * 4 + me.x
    core = me.core

    def tp_mate(dx, dy):
        return lax.rem(me.x + dx, 4), lax.rem(low + dy, 2)

    def idx_mate(dz, dy):
        return me.device(z=lax.rem(me.z + dz, 4), y=lax.rem(high + dy, 2) * 2 + low)

    others = [me.device(x=x, y=high * 2 + y) for x, y in (tp_mate(*d) for d in OTHERS_TP)]
    far = [idx_mate(*d) for d in OTHERS_IDX]
    greet([me.next_to(a, t) for a, t in LINKS] + [me.mate()] + others + far)

    def remote(src, dst, s, r, device):
        return pltpu.make_async_remote_copy(src_ref=src, dst_ref=dst, send_sem=s, recv_sem=r,
                                            device_id=device, device_id_type=MESH)

    to_mate = remote(part_ref.at[:, 1 - core], from_mate, mate_sem.at[0], mate_sem.at[1], me.mate())
    to_mate.start()
    shard = lax.axis_index("idx")
    count_copies = []
    for n, device in enumerate(far):
        copy = remote(counts_ref, their_counts.at[shard], c_out.at[n], c_in.at[n], device)
        copy.start()
        count_copies.append(copy)

    def columns(x, y_low):
        block = lax.rem(me.z, 2) * 16 + (high * 2 + y_low) * 4 + x
        return f_hbm.at[:, pl.ds(pl.multiple_of(block * 128, 128), 128)]

    place = me.x * 2 + low
    f_copies = []
    for n, d in enumerate(OTHERS_TP):
        f_copies.append(remote(columns(*tp_mate(*d)), fisher.at[place, core], f_out.at[n], f_in.at[n], others[n]))
    own_f = pltpu.make_async_copy(columns(me.x, low), fisher.at[place, core], f_own)
    own_f.start()

    to_mate.wait()
    for q in range(8):
        mine[q] = part_ref[q, core] + from_mate[q]
    arrived[p] = mine[p]
    rs_copies = []
    for n, d in enumerate(OTHERS_TP):
        x, y = tp_mate(*d)
        copy = remote(mine.at[y * 4 + x], arrived.at[p], rs_out.at[n], rs_in.at[n], others[n])
        copy.start()
        rs_copies.append(copy)
    for copy in f_copies:
        copy.start()
    for copy in rs_copies:
        copy.wait_recv()
    total = arrived[0]
    for q in range(1, 8):
        total = total + arrived[q]
    gather = Gather(me, bufs, sems)
    for k in range(COLOURS):
        own = gather.boxes[k][0]
        for u in range(T_UNITS[k]):
            row = (T_FIRST[k] + u) * 4
            bufs[k][core, own["z"][0], own["y"][0], own["x"][0], u] = total[row:row + 4]
    gather.start()

    their_counts[shard] = counts_ref[...]
    for copy in count_copies:
        copy.wait_recv()
    summed = their_counts[0]
    for n in range(1, 8):
        summed = summed + their_counts[n]
    counts_sum[...] = summed
    to_scalar = pltpu.make_async_copy(counts_sum, counts, c_sem)
    to_scalar.start()
    to_scalar.wait()

    for s in range(1, 6):
        gather.step(s)
        if s == 4:
            own_f.wait()
            for copy in f_copies:
                copy.wait_recv()
            pass_f = remote(fisher.at[:, core], fisher.at[:, core], f_pass.at[0], f_pass.at[1], me.mate())
            pass_f.start()
    for b in range(6):
        gather.last(b)
    for n in range(PASSES):
        gather.from_mate(n)

    @pl.loop(0, 64)
    def _(chip):
        z, y, x = chip // 16, lax.rem(chip // 4, 4), lax.rem(chip, 4)
        for c in range(2):
            base = pl.multiple_of(chip * 128 + c * 64, 64)
            for k in range(COLOURS):
                for u in range(T_UNITS[k]):
                    tok[pl.ds(base + (T_FIRST[k] + u) * 4, 4), :] = bufs[k][
                        c, spot(z, turned(k, "z")), spot(y, turned(k, "y")), spot(x, turned(k, "x")), u]

    tok[8192:8224, :] = jnp.zeros((32, 128), F32)

    first_row = (core * 2 + me.z // 2) * 256
    lane = lax.broadcasted_iota(jnp.int32, (128, 128), 1)
    sub = lax.broadcasted_iota(jnp.int32, (32, 128), 0)
    same = lax.broadcasted_iota(jnp.int32, (128, 256), 0) // 32 == lax.rem(
        lax.broadcasted_iota(jnp.int32, (128, 256), 1), 128) // 32

    @pl.loop(0, 64)
    def _(group):
        rows = []
        for q in range(4):
            r = first_row + group * 4 + q
            start = counts[r // 128, lax.rem(r, 128)]
            length = counts[8 + r // 128, lax.rem(r, 128)]
            rows.append(jnp.where(sub < length, tok[pl.ds(start, 32), :], 0.0))
        pieces = jnp.concatenate(rows, 0)
        turned_pieces = pieces.T
        lead = jnp.concatenate([turned_pieces[64:96], turned_pieces[96:128]], 1)
        lead = jnp.where(same, jnp.concatenate([lead] * 4, 0), 0.0)
        lead_high, lead_low = halves(lead)
        top = jnp.where(lane < 64, pieces, 0.0)
        bottom = jnp.where(lane < 64, 0.0, pltpu.roll(pieces, 64, 1))
        right_high, right_low = halves(jnp.concatenate([top, bottom], 0))
        both = jnp.dot(lead_high, jnp.concatenate([right_high, right_low], 1), preferred_element_type=F32)
        rest = jnp.dot(lead_low, right_high, preferred_element_type=F32)
        got = both[:, :128] + both[:, 128:] + rest
        for q in range(4):
            dg[pl.ds(group * 4 + q, 32, stride=PITCH), :] = got[q * 32:(q + 1) * 32]

    pass_f.wait_recv()
    acc[...] = jnp.zeros_like(acc)
    lacc[...] = jnp.zeros_like(lacc)

    @pl.loop(0, 16)
    def _(kk):
        left = dg[pl.ds(pl.multiple_of(kk * 2 * PITCH, 8), 256), :]
        right = dg[pl.ds(pl.multiple_of((kk * 2 + 1) * PITCH, 8), 256), :]
        d_high, d_low = halves(jnp.concatenate([left, right], 1))
        f_high, f_low = halves(fisher[kk // 2, lax.rem(kk, 2)])
        acc[...] += jnp.dot(d_high, jnp.concatenate([f_high, f_low], 1), preferred_element_type=F32)
        lacc[...] += jnp.dot(d_low, f_high, preferred_element_type=F32)

    result = acc[:, :128] + acc[:, 128:] + lacc[...]
    out_ref[...] = result.astype(BF16).reshape(16, 16, 128)

    for copy in count_copies + f_copies + rs_copies + [pass_f]:
        copy.wait_send()
    gather.close()


def queries_call(part, inv_fisher, counts):
    vmem = pl.BlockSpec(memory_space=pltpu.VMEM)
    dma = pltpu.SemaphoreType.DMA
    return pl.pallas_call(
        queries_kernel,
        out_shape=jax.ShapeDtypeStruct((16, 16, 128), BF16),
        in_specs=[vmem, pl.BlockSpec(memory_space=pl.ANY), vmem],
        out_specs=vmem,
        scratch_shapes=[
            pltpu.VMEM((8, 64, 128), F32), pltpu.VMEM((8, 64, 128), F32), pltpu.VMEM((8, 64, 128), F32)]
        + [pltpu.VMEM((2, 4, 4, 4, n, 4, 128), F32) for n in T_UNITS]
        + [pltpu.VMEM((8224, 128), F32), pltpu.VMEM((8, 2, 256, 128), F32),
           pltpu.VMEM((8, 16, 128), jnp.int32), pltpu.VMEM((16, 128), jnp.int32), pltpu.SMEM((16, 128), jnp.int32),
           pltpu.VMEM((32 * PITCH, 128), F32), pltpu.VMEM((256, 256), F32), pltpu.VMEM((256, 128), F32),
           dma((2,)), dma((7,)), dma((7,)), dma((7,)), dma((7,)), dma((2,)), dma, dma((7,)), dma((7,)), dma]
        + Gather.semaphores(),
        compiler_params=pltpu.CompilerParams(collective_id=2, has_side_effects=True, vmem_limit_bytes=48 << 20),
        name="queries",
    )(part, inv_fisher, counts)


def per_device(activations, out_grads, proj_in, proj_out, doc_ids, doc_order, inv_fisher, index_grads):
    lead_pairs = proj_out.reshape(-1, 32, 2).transpose(0, 2, 1).reshape(-1, 64)
    part = jnp.concatenate([
        jnp.dot(activations, proj_in, preferred_element_type=F32),
        jnp.dot(out_grads, lead_pairs, preferred_element_type=F32)], 1)
    before = jnp.sum((doc_ids[:, None] < doc_order[None, :]).astype(jnp.int32), 0)
    equal = jnp.sum((doc_ids[:, None] == doc_order[None, :]).astype(jnp.int32), 0)
    counts = jnp.concatenate([before.reshape(8, 128), equal.reshape(8, 128)], 0)
    block = queries_call(part.reshape(8, 2, 64, 128), inv_fisher, counts)
    return scores_call(block, index_grads)


def solution(mesh):
    placed = (
        P("idx", "tp"), P("idx", "tp"), P("tp", None), P("tp", None),
        P("idx"), P(), P("tp", None), P(("idx", "tp"), None),
    )
    return jax.shard_map(
        per_device, mesh=mesh, in_specs=placed, out_specs=P(None, ("idx", "tp")), check_vma=False)
```

time: 328 us -> 138 us (0.42)
  waiting for transfers between devices: 207 us -> 0 us
  Pallas kernels: 0 us -> 127 us
  blocking collectives: 71 us -> 0 us
  matrix products: 25.2 us -> 3.7 us
  between operations: 13.5 us -> 0.08 us
  starting transfers between devices: 4.62 us -> 0 us
    all_gather x1 -> x0, waiting for transfers between devices: 198 us -> none  [per_device(): lax.all_gather(queries, ('idx', 'tp'), axis=0, tiled=True)]
    pallas_call x0 -> x2, Pallas kernels: none -> 127 us  [the longest x1 78 us: queries_call(): pl.pallas_call(queries_kernel, out_shape=jax.ShapeDtypeStruct((16, 16, 12...]
    all_to_all x3 -> x0, blocking collectives: 71 us -> none  [summed_on_arrival(): blocks = lax.all_to_all(cut_along(value, dim, size), axis, 0, 0, tiled=True)]
    dot_general x5 -> x2, matrix products: 25.2 us -> 3.7 us  [the longest x1 3.26 us: per_device(): jnp.dot(activations, proj_in, preferred_element_type=F32)]
    all_to_all x1 -> x0, waiting for transfers between devices: 9.71 us -> none  [copy_for_each(): return lax.all_to_all(copies, axis, split_axis=0, concat_axis=0, tiled=True)]
    all_to_all x1 -> x0, starting transfers between devices: 4.59 us -> none  [copy_for_each(): return lax.all_to_all(copies, axis, split_axis=0, concat_axis=0, tiled=True)]
    unnamed x8 -> x5, local copies, waits for them, and re-layouts: 0.02 us -> 4.21 us
  transfers between devices with their start and end apart: 2 -> 0, of which waited for: 2 -> 0; matrix products, arithmetic and copies ran while one was open for 0% -> 0% of each run, Pallas kernels for 0% -> 0%
where the time goes in v1:
time: 138 us; the launch traced here: 137 us
  Pallas kernels  127 us (92%)
  local copies, waits for them, and re-layouts  5.28 us (4%)
  matrix products  3.7 us (3%)
  other arithmetic  1.73 us (1%)
    pallas_call x1, Pallas kernels, queries_call(): pl.pallas_call(queries_kernel, out_shape=jax.ShapeDtypeStruct((16, 16, 12...  78 us
    pallas_call x1, Pallas kernels, scores_call(): pl.pallas_call(scores_kernel, out_shape=jax.ShapeDtypeStruct((1024, 1024)...  48.6 us
    unnamed x5, local copies, waits for them, and re-layouts  4.21 us
    dot_general x1, matrix products, per_device(): jnp.dot(activations, proj_in, preferred_element_type=F32)  3.26 us

profile of v1, /device:TPU:1, one launch (start us, length us, event | category | flops | bytes accessed | tf_op | source)
XLA Modules:
  0.0 137.4 jit_solution(18199541305057233007)
XLA Ops:
  0.0 0.0 copy-start
  0.0 1.7 %convert_reduce_fusion.1 = (s32[1024]{0:T(1024)S(1)}, s32[1024]{0:T(1024)S(1)}) fusion(s32[1024]{0:T(1024)} %param.13, s32[1024]{0:T(1024)} %param.12), kind=kLoop, calls=%fused_computation.1 | loop fusion | flops 6289408 | bytes 16384 | tf_op jit(solution)/shard_map/reduce_sum | solution.py:426
  1.7 0.9 reshape.17
  2.6 0.0 copy-done
  2.6 0.4 fusion.1
  3.0 3.3 %fusion = f32[1024,64]{0,1:T(8,128)S(1)} fusion(bf16[1024,1792]{1,0:T(8,128)(2,1)} %param.8, bf16[1792,64]{0,1:T(8,128)(2,1)} %param.10), kind=kOutput, calls=%fused_computation.4 | convolution fusion | flops 234881024 | bytes 4161536 | tf_op jit(solution)/shard_map/dot_general | solution.py:424
  6.3 0.1 pad_maximum_fusion
  6.4 0.2 copy.14
  6.6 0.0 copy-start.1
  6.6 2.2 %copy-done.1 = f32[256,4096]{1,0:T(8,128)S(1)} copy-done((f32[256,4096]{1,0:T(8,128)S(1)}, f32[256,4096]{1,0:T(8,128)}, u32[]{:S(2)}) %copy-start.1) | copy-done | bytes 4194328
  8.8 78.0 %queries.1.blk_ref = bf16[16,16,128]{2,1,0:T(8,128)(2,1)S(1)} custom-call(f32[8,2,64,128]{3,2,1,0:T(8,128)S(1)} %bitcast.11, f32[256,4096]{1,0:T(8,128)S(1)} %copy-done.1, s32[16,128]{1,0:T(8,128)S(1)} %pad_add_fusion.counts_ref), custom_call_target="tpu_custom_call" | custom-call | tf_op jit(solution)/shard_map/queries/pallas_call | solution.py:403
  86.8 48.6 %scores.1 = f32[1024,1024]{1,0:T(8,128)S(1)} custom-call(bf16[16,16,128]{2,1,0:T(8,128)(2,1)S(1)} %queries.1.blk_ref, bf16[1024,4096]{1,0:T(8,128)(2,1)} %g_hbm.1), custom_call_target="tpu_custom_call" | custom-call | tf_op jit(solution)/shard_map/scores/pallas_call | solution.py:221
  135.4 2.0 %copy.16 = f32[1024,1024]{1,0:T(8,128)} copy(f32[1024,1024]{1,0:T(8,128)S(1)} %scores.1) | data formatting | bytes 8388608
  (2 shorter events, 0.0 us)
Async XLA Ops:
  0.0 2.6 %copy-start = (bf16[1024,512]{1,0:T(8,128)(2,1)S(1)}, bf16[1024,512]{1,0:T(8,128)(2,1)}, u32[]{:S(2)}) copy-start(bf16[1024,512]{1,0:T(8,128)(2,1)} %param.9) | copy-start | bytes 3145732
  6.6 2.2 %copy-start.1 = (f32[256,4096]{1,0:T(8,128)S(1)}, f32[256,4096]{1,0:T(8,128)}, u32[]{:S(2)}) copy-start(f32[256,4096]{1,0:T(8,128)} %f_hbm.1) | copy-start | bytes 12582916

commit v2 on v0

v2 whole, which is shorter than its diff:
```python
import functools

import jax
import jax.numpy as jnp
from jax import lax
from jax.experimental import pallas as pl
from jax.experimental.pallas import tpu as pltpu
from jax.sharding import PartitionSpec as P

MESH = pl.DeviceIdType.MESH
F32, BF16 = jnp.float32, jnp.bfloat16
LINKS = (("x", 0), ("y", 0), ("z", 0), ("x", 1), ("y", 1), ("z", 1))
COLOURS = 6


class Place:
    def __init__(self):
        idx, tp = lax.axis_index("idx"), lax.axis_index("tp")
        self.x, self.z = tp // 4, idx // 2
        self.y = lax.rem(idx, 2) * 2 + lax.rem(tp // 2, 2)
        self.core = lax.rem(tp, 2)

    def device(self, x=None, y=None, z=None, core=None):
        x = self.x if x is None else x
        y = self.y if y is None else y
        z = self.z if z is None else z
        core = self.core if core is None else core
        return (z * 2 + y // 2, (x * 2 + lax.rem(y, 2)) * 2 + core)

    def across(self, axis, kind):
        v = getattr(self, axis)
        if kind:
            return lax.rem(v + 3 + 2 * lax.rem(v, 2), 4)
        return v + 1 - 2 * lax.rem(v, 2)

    def mate(self):
        return self.device(core=1 - self.core)

    def next_to(self, axis, kind):
        return self.device(**{axis: self.across(axis, kind)})


SUBSETS = [tuple(s for s in (0, 1, 2) if n >> s & 1) for n in (0, 1, 2, 4, 3, 5, 6, 7)]
OCTETS = [(), (3,), (4,), (3, 4), (5,), (3, 5), (4, 5), (3, 4, 5)]


def order_of(colour):
    return [LINKS[(colour + s) % 6] for s in range(6)]


def turned(colour, axis):
    order = order_of(colour)
    return 1 if order.index((axis, 1)) < order.index((axis, 0)) else 0


def spot(v, turn):
    return lax.rem(v + 3 * turn, 4)


class Gather:
    def __init__(self, me, bufs, sems):
        self.me, self.bufs = me, bufs
        self.out_sem, self.in_sem, self.pass_out, self.pass_in = sems
        self.places = {}
        for axis in "xyz":
            for turn in range(2):
                p = spot(getattr(me, axis), turn)
                over = lax.rem(p + 3 + 2 * lax.rem(p, 2), 4)
                for crossed, base in enumerate((p, over)):
                    self.places[axis, turn, 0, crossed] = base
                    self.places[axis, turn, 1, crossed] = base + 1 - 2 * lax.rem(base, 2)

    @staticmethod
    def semaphores():
        dma = pltpu.SemaphoreType.DMA
        return [dma((COLOURS, 15)), dma((COLOURS, 16)), dma((COLOURS, 8)), dma((COLOURS, 8))]

    def at(self, k, subset, octet):
        order = order_of(k)
        got = []
        for axis in "zyx":
            flip = any(order[s][0] == axis for s in subset)
            crossed = any(order[s][0] == axis for s in octet)
            got.append(self.places[axis, turned(k, axis), int(flip), int(crossed)])
        return got

    def cell(self, k, octet):
        got = []
        for axis in "zyx":
            crossed = any(order_of(k)[s][0] == axis for s in octet)
            base = self.places[axis, turned(k, axis), 0, int(crossed)]
            got.append(base - lax.rem(base, 2))
        return got

    def cell_ref(self, k, core, octet):
        z, y, x = self.cell(k, octet)
        return self.bufs[k].at[core, pl.ds(z, 2), pl.ds(y, 2), pl.ds(x, 2)]

    def send(self, k, ref, out, into, device):
        return pltpu.make_async_remote_copy(
            src_ref=ref, dst_ref=ref, send_sem=self.out_sem.at[k, out], recv_sem=self.in_sem.at[k, into],
            device_id=device, device_id_type=MESH)

    def direct(self, k, n):
        move = {}
        for s in SUBSETS[n]:
            axis, kind = order_of(k)[s]
            move[axis] = self.me.across(axis, kind)
        ref = self.bufs[k].at[(self.me.core, *self.at(k, (), ()))]
        return self.send(k, ref, n, n, self.me.device(**move))

    def onward(self, k, step, octet):
        axis, kind = order_of(k)[step]
        reached = OCTETS.index(octet + (step,))
        return self.send(k, self.cell_ref(k, self.me.core, octet), 7 + reached, 8 + reached,
                         self.me.next_to(axis, kind))

    def arrive(self, k, octet):
        if octet:
            ref = self.cell_ref(k, self.me.core, octet)
            self.send(k, ref, 0, 8 + OCTETS.index(octet), self.me.mate()).wait_recv()
            return
        for n in range(1, 8):
            ref = self.bufs[k].at[(self.me.core, *self.at(k, SUBSETS[n], ()))]
            self.send(k, ref, 0, n, self.me.mate()).wait_recv()

    def passed(self, k, octet, core):
        n = OCTETS.index(octet)
        ref = self.cell_ref(k, core, octet)
        return pltpu.make_async_remote_copy(
            src_ref=ref, dst_ref=ref, send_sem=self.pass_out.at[k, n], recv_sem=self.pass_in.at[k, n],
            device_id=self.me.mate(), device_id_type=MESH)

    def start(self):
        for n in range(1, 8):
            for k in range(COLOURS):
                self.direct(k, n).start()

    def forward(self, step, octet):
        for k in range(COLOURS):
            self.onward(k, step, octet).start()

    def take(self, octet):
        step = max((2,) + octet) + 1
        for k in range(COLOURS):
            self.arrive(k, octet)
            if step < 6:
                self.onward(k, step, octet).start()
        if octet == ():
            self.forward(4, ())
        if octet == (3,):
            self.forward(5, ())
            self.forward(5, (3,))
        for k in range(COLOURS):
            self.passed(k, octet, self.me.core).start()

    def from_mate(self, octet):
        for k in range(COLOURS):
            self.passed(k, octet, 1 - self.me.core).wait_recv()

    def close(self):
        for k in range(COLOURS):
            for n in range(1, 8):
                self.direct(k, n).wait_send()
            for octet in OCTETS:
                for step in range(max((2,) + octet) + 1, 6):
                    self.onward(k, step, octet).wait_send()
                self.passed(k, octet, self.me.core).wait_send()


def cell_mates(me):
    found = {}
    for k in range(COLOURS):
        for subset in SUBSETS[1:]:
            steps = tuple(sorted(order_of(k)[n] for n in subset))
            found[steps] = me.device(**{axis: me.across(axis, kind) for axis, kind in steps})
    return list(found.values()) + [me.mate()]


def remote(src, dst, s, r, device):
    return pltpu.make_async_remote_copy(
        src_ref=src, dst_ref=dst, send_sem=s, recv_sem=r, device_id=device, device_id_type=MESH)


def halves(v):
    high = v.astype(BF16)
    return high, (v - high.astype(F32)).astype(BF16)


UNITS = (3, 3, 3, 3, 2, 2)
FIRST = (0, 3, 6, 9, 12, 14)
T_UNITS = (2, 1, 1, 2, 1, 1)
T_FIRST = (0, 2, 3, 4, 6, 7)
OTHERS_TP = [(dx, dy) for dx in range(4) for dy in range(2)][1:]
OTHERS_IDX = [(dz, dy) for dz in range(4) for dy in range(2)][1:]
PITCH = 264
LANES = (((1,), (1,)), ((), ()))


def multiply(gather, k, crossed, bufs, gt_ref, out_ref):
    rows = UNITS[k] * 16
    lows = {}
    for step, over in crossed.items():
        axis = order_of(k)[step][0]
        low = gather.places[axis, turned(k, axis), 0, over]
        lows[axis] = low - lax.rem(low, 2)

    def spots_of(axis):
        return [lows[axis] + n for n in range(2)] if axis in lows else list(range(4))

    def natural(p, a):
        return lax.rem(p + turned(k, a), 4)

    def product(spots, out_rows):
        starts = []
        for _, z, y, x in spots[0]:
            zn, yn, xn = natural(z, "z"), natural(y, "y"), natural(x, "x")
            starts.append(pl.multiple_of((lax.rem(zn, 2) * 16 + yn * 4 + xn) * 128, 128))
        lhs = jnp.concatenate([
            jnp.concatenate([bufs[k][s].reshape(rows, 128) for s in blocks], 1) for blocks in spots], 0)
        for tile in range(4):
            cols = pl.ds(tile * 256, 256)
            rhs = jnp.concatenate([gt_ref[pl.ds(start, 128), cols] for start in starts], 0)
            got = jnp.dot(lhs, rhs, preferred_element_type=F32)
            for n, row in enumerate(out_rows):
                where = pl.ds(pl.multiple_of(row + FIRST[k] * 16, 16), rows)
                out_ref[where, cols] += got[n * rows:(n + 1) * rows]

    if "z" in lows:
        @pl.loop(0, 2)
        def _(n):
            z = lows["z"] + n
            high = natural(z, "z") // 2
            pairs = [(y, x) for y in spots_of("y") for x in spots_of("x")]
            for first in range(0, len(pairs), 8):
                product([[(core, z, y, x) for y, x in pairs[first:first + 8]] for core in range(2)],
                        [(core * 2 + high) * 256 for core in range(2)])
        return

    @pl.loop(0, 2)
    def _(z_low):
        pairs = [(y, x) for y in spots_of("y") for x in spots_of("x")]
        blocks, out_rows = [], []
        for core in range(2):
            for high in range(2):
                z = spot(high * 2 + z_low, turned(k, "z"))
                blocks.append([(core, z, y, x) for y, x in pairs])
                out_rows.append((core * 2 + high) * 256)
        product(blocks, out_rows)


def kernel(
    act_hbm, og_hbm, pin_hbm, pout_hbm, ids_hbm, order_hbm, f_hbm, g_hbm, out_ref,
    ids_ref, order_ref, act, og, pin, pout, part, from_mate, mine, arrived, t0, t1, t2, t3, t4, t5, tok, fisher,
    counts_ref, their_counts, counts_sum, counts, dg, acc, lacc, q0, q1, q2, q3, q4, q5, g_ref, gt_ref,
    load_sem, mate_sem, rs_out, rs_in, f_out, f_in, f_pass, f_own, c_out, c_in, c_sem, g_sem, *sems):
    me = Place()
    bufs, qbufs = (t0, t1, t2, t3, t4, t5), (q0, q1, q2, q3, q4, q5)
    low, high, core = lax.rem(me.y, 2), me.y // 2, me.core
    p = low * 4 + me.x
    place = me.x * 2 + low

    def tp_mate(dx, dy):
        return lax.rem(me.x + dx, 4), lax.rem(low + dy, 2)

    def idx_mate(dz, dy):
        return me.device(z=lax.rem(me.z + dz, 4), y=lax.rem(high + dy, 2) * 2 + low)

    others = [me.device(x=x, y=high * 2 + y) for x, y in (tp_mate(*d) for d in OTHERS_TP)]
    far = [idx_mate(*d) for d in OTHERS_IDX]

    loads = [pltpu.make_async_copy(s, d, load_sem.at[n]) for n, (s, d) in enumerate(
        ((ids_hbm, ids_ref), (order_hbm, order_ref), (pin_hbm, pin), (act_hbm, act), (pout_hbm, pout), (og_hbm, og)))]
    for load in loads:
        load.start()

    def columns(x, y_low):
        block = lax.rem(me.z, 2) * 16 + (high * 2 + y_low) * 4 + x
        return f_hbm.at[:, pl.ds(pl.multiple_of(block * 128, 128), 128)]

    own_f = pltpu.make_async_copy(columns(me.x, low), fisher.at[place, core], f_own)
    own_f.start()
    friends = cell_mates(me) + others + far
    barrier = pltpu.get_barrier_semaphore()
    for device in friends:
        pl.semaphore_signal(barrier, inc=1, device_id=device, device_id_type=MESH)

    loads[0].wait()
    loads[1].wait()
    ids = jnp.concatenate([ids_ref[...]] * 16, 0).T
    less, same_doc = [0] * 8, [0] * 8
    for c in range(8):
        column = jnp.broadcast_to(ids[:, c:c + 1], (128, 128))
        for r in range(8):
            wanted = jnp.broadcast_to(order_ref[r:r + 1, :], (128, 128))
            below = jnp.where(column < wanted, 1, 0).reshape(16, 8, 128)
            equal = jnp.where(column == wanted, 1, 0).reshape(16, 8, 128)
            less[r] = less[r] + jnp.sum(below, 0)
            same_doc[r] = same_doc[r] + jnp.sum(equal, 0)
    for r in range(8):
        counts_ref[r:r + 1, :] = jnp.sum(less[r], 0, keepdims=True)
        counts_ref[8 + r:9 + r, :] = jnp.sum(same_doc[r], 0, keepdims=True)
    for load in loads[2:]:
        load.wait()
    def load_g(n):
        cols = pl.ds(n * 512, 512)
        return pltpu.make_async_copy(g_hbm.at[:, cols], g_ref.at[n % 2], g_sem.at[n % 2])

    load_g(0).start()
    load_g(1).start()

    @pl.loop(0, 4)
    def _(n):
        rows = pl.ds(pl.multiple_of(n * 256, 256), 256)
        both = jnp.concatenate([
            lax.dot_general(act[rows, :], pin[...], LANES, preferred_element_type=F32),
            lax.dot_general(og[rows, :], pout[...], LANES, preferred_element_type=F32)], 1)
        part[pl.ds(n * 2, 2)] = both.reshape(2, 2, 64, 128)

    pl.semaphore_wait(barrier, len(friends))

    shard = lax.axis_index("idx")
    count_copies = []
    for n, device in enumerate(far):
        copy = remote(counts_ref, their_counts.at[shard], c_out.at[n], c_in.at[n], device)
        copy.start()
        count_copies.append(copy)
    f_copies = []
    for n, d in enumerate(OTHERS_TP):
        f_copies.append(remote(columns(*tp_mate(*d)), fisher.at[place, core], f_out.at[n], f_in.at[n], others[n]))

    to_mate = remote(part.at[:, 1 - core], from_mate, mate_sem.at[0], mate_sem.at[1], me.mate())
    to_mate.start()
    to_mate.wait()
    rs_copies = []
    for q in range(8):
        mine[q] = part[q, core] + from_mate[q]
    arrived[p] = mine[p]
    for n, d in enumerate(OTHERS_TP):
        x, y = tp_mate(*d)
        copy = remote(mine.at[y * 4 + x], arrived.at[p], rs_out.at[n], rs_in.at[n], others[n])
        copy.start()
        rs_copies.append(copy)

    their_counts[shard] = counts_ref[...]
    for copy in count_copies:
        copy.wait_recv()
    summed = their_counts[0]
    for n in range(1, 8):
        summed = summed + their_counts[n]
    counts_sum[...] = summed
    to_scalar = pltpu.make_async_copy(counts_sum, counts, c_sem)
    to_scalar.start()
    to_scalar.wait()


    def turn(*chunks):
        for n in chunks:
            load_g(n).wait()

            @pl.loop(0, 4)
            def _(block):
                cols = pl.ds(pl.multiple_of(block * 128, 128), 128)
                gt_ref[pl.ds(pl.multiple_of(n * 512 + block * 128, 128), 128), :] = g_ref[n % 2, :, cols].T

            if n < 6:
                load_g(n + 2).start()

    turn(0, 1)
    for copy in rs_copies:
        copy.wait_recv()
    total = arrived[0]
    for q in range(1, 8):
        total = total + arrived[q]
    gather = Gather(me, bufs, sems[:4])
    for k in range(COLOURS):
        own = gather.at(k, (), ())
        row = T_FIRST[k] * 8
        bufs[k][(core, *own)] = total[row:row + T_UNITS[k] * 8].reshape(T_UNITS[k], 8, 128)
    gather.start()
    for n in EARLY_F:
        f_copies[n].start()
    turn(2, 3, 4)

    def spread(octet):
        for k in range(COLOURS):
            z0, y0, x0 = gather.cell(k, octet)
            zs, ys, xs = ([lax.rem(v + n + turned(k, a), 4) for n in range(2)]
                          for a, v in (("z", z0), ("y", y0), ("x", x0)))
            for n in range(8):
                a, b, c = n // 4, n // 2 % 2, n % 2
                chip = zs[a] * 16 + ys[b] * 4 + xs[c]
                for side in range(2):
                    base = pl.multiple_of(chip * 128 + side * 64 + T_FIRST[k] * 8, 8)
                    tok[pl.ds(base, T_UNITS[k] * 8), :] = bufs[k][side, z0 + a, y0 + b, x0 + c].reshape(
                        T_UNITS[k] * 8, 128)

    tok[8192:8224, :] = jnp.zeros((32, 128), F32)
    for n, octet in enumerate(OCTETS):
        gather.take(octet)
        if n == 0:
            turn(5, 6, 7)
        if n:
            gather.from_mate(OCTETS[n - 1])
            spread(OCTETS[n - 1])
        if n == 1:
            for m in LATE_F:
                f_copies[m].start()
        if n == 3:
            for m in LAST_F:
                f_copies[m].start()
    gather.from_mate(OCTETS[7])
    spread(OCTETS[7])

    first_row = (core * 2 + me.z // 2) * 256
    lane = lax.broadcasted_iota(jnp.int32, (128, 128), 1)
    sub = lax.broadcasted_iota(jnp.int32, (32, 128), 0)
    same = lax.broadcasted_iota(jnp.int32, (128, 256), 0) // 32 == lax.rem(
        lax.broadcasted_iota(jnp.int32, (128, 256), 1), 128) // 32

    def sum_tokens(group):
        rows = []
        for q in range(4):
            r = first_row + group * 4 + q
            start = counts[r // 128, lax.rem(r, 128)]
            length = counts[8 + r // 128, lax.rem(r, 128)]
            rows.append(jnp.where(sub < length, tok[pl.ds(start, 32), :], 0.0))
        pieces = jnp.concatenate(rows, 0)
        lead = pieces.T
        lead = jnp.concatenate([lead[64:96], lead[96:128]], 1)
        lead = jnp.where(same, jnp.concatenate([lead] * 4, 0), 0.0)
        lead_high, lead_low = halves(lead)
        top = jnp.where(lane < 64, pieces, 0.0)
        bottom = jnp.where(lane < 64, 0.0, pltpu.roll(pieces, 64, 1))
        right_high, right_low = halves(jnp.concatenate([top, bottom], 0))
        both = jnp.dot(lead_high, jnp.concatenate([right_high, right_low], 1), preferred_element_type=F32)
        rest = jnp.dot(lead_low, right_high, preferred_element_type=F32)
        got = both[:, :128] + both[:, 128:] + rest
        for q in range(4):
            dg[pl.ds(group * 4 + q, 32, stride=PITCH), :] = got[q * 32:(q + 1) * 32]

    pl.loop(0, 32, unroll=8)(sum_tokens)
    own_f.wait()
    for copy in f_copies:
        copy.wait_recv()
    pass_f = remote(fisher.at[:, core], fisher.at[:, core], f_pass.at[0], f_pass.at[1], me.mate())
    pass_f.start()
    pl.loop(32, 64, unroll=8)(sum_tokens)
    pass_f.wait_recv()
    acc[...] = jnp.zeros_like(acc)
    lacc[...] = jnp.zeros_like(lacc)

    @pl.loop(0, 16, unroll=4)
    def _(kk):
        left = dg[pl.ds(pl.multiple_of(kk * 2 * PITCH, 8), 256), :]
        right = dg[pl.ds(pl.multiple_of((kk * 2 + 1) * PITCH, 8), 256), :]
        d_high, d_low = halves(jnp.concatenate([left, right], 1))
        tiles = []
        for n in range(2):
            for half in range(2):
                lead = kk * 2 + n + half * 32
                tiles.append(fisher[lead // 8, lax.rem(lead // 4, 2), pl.ds(pl.multiple_of(
                    lax.rem(lead, 4) * 64, 64), 64), :])
        f_high, f_low = halves(jnp.concatenate(tiles, 0))
        acc[...] += jnp.dot(d_high, jnp.concatenate([f_high, f_low], 1), preferred_element_type=F32)
        lacc[...] += jnp.dot(d_low, f_high, preferred_element_type=F32)

    block = (acc[:, :128] + acc[:, 128:] + lacc[...]).astype(BF16)
    scores = Gather(me, qbufs, sems[4:])
    for k in range(COLOURS):
        first = FIRST[k] * 16
        qbufs[k][(core, *scores.at(k, (), ()))] = block[first:first + UNITS[k] * 16].reshape(UNITS[k], 16, 128)
    scores.start()
    out_ref[...] = jnp.zeros_like(out_ref)
    for octet in OCTETS[:4]:
        scores.take(octet)
    for octet in OCTETS[:4]:
        scores.from_mate(octet)
    for n, octet in enumerate(OCTETS[4:]):
        for k in range(2 * n, min(2 * n + 2, COLOURS)):
            multiply(scores, k, {5: 0}, qbufs, gt_ref, out_ref)
        if n < 3:
            scores.take(octet)
    for octet in OCTETS[4:6]:
        scores.from_mate(octet)
    for k in range(COLOURS):
        multiply(scores, k, {4: 0, 5: 1}, qbufs, gt_ref, out_ref)
        if k == 3:
            scores.take(OCTETS[7])
    for octet in OCTETS[6:]:
        scores.from_mate(octet)
    for k in range(COLOURS):
        multiply(scores, k, {4: 1, 5: 1}, qbufs, gt_ref, out_ref)

    for copy in count_copies + f_copies + rs_copies + [pass_f]:
        copy.wait_send()
    gather.close()
    scores.close()


EARLY_F = (0, 1, 5)
LATE_F = (2, 6)
LAST_F = (3, 4)


def per_device(activations, out_grads, proj_in, proj_out, doc_ids, doc_order, inv_fisher, index_grads):
    vmem, hbm = pl.BlockSpec(memory_space=pltpu.VMEM), pl.BlockSpec(memory_space=pltpu.HBM)
    dma = pltpu.SemaphoreType.DMA
    scratch = [pltpu.VMEM((8, 128), jnp.int32), pltpu.VMEM((8, 128), jnp.int32)]
    scratch += [pltpu.VMEM((1024, 1792), BF16), pltpu.VMEM((1024, 512), BF16), pltpu.VMEM((64, 1792), BF16),
               pltpu.VMEM((64, 512), BF16), pltpu.VMEM((8, 2, 64, 128), F32)]
    scratch += [pltpu.VMEM((8, 64, 128), F32)] * 3
    scratch += [pltpu.VMEM((2, 4, 4, 4, n, 8, 128), F32) for n in T_UNITS]
    scratch += [pltpu.VMEM((8224, 128), F32), pltpu.VMEM((8, 2, 256, 128), F32),
                pltpu.VMEM((16, 128), jnp.int32), pltpu.VMEM((8, 16, 128), jnp.int32),
                pltpu.VMEM((16, 128), jnp.int32), pltpu.SMEM((16, 128), jnp.int32),
                pltpu.VMEM((32 * PITCH, 128), F32), pltpu.VMEM((256, 256), F32), pltpu.VMEM((256, 128), F32)]
    scratch += [pltpu.VMEM((2, 4, 4, 4, n, 16, 128), BF16) for n in UNITS]
    scratch += [pltpu.VMEM((2, 1024, 512), BF16), pltpu.VMEM((4096, 1024), BF16)]
    scratch += [dma((6,)), dma((2,)), dma((7,)), dma((7,)), dma((7,)), dma((7,)), dma((2,)), dma, dma((7,)), dma((7,)),
                dma, dma((2,))]
    return pl.pallas_call(
        kernel,
        out_shape=pltpu.VMEM((1024, 1024), F32),
        in_specs=[hbm] * 8,
        out_specs=vmem,
        scratch_shapes=scratch + Gather.semaphores() + Gather.semaphores(),
        compiler_params=pltpu.CompilerParams(collective_id=2, has_side_effects=True, vmem_limit_bytes=46 << 20),
        name="influence",
    )(*(pltpu.with_memory_space_constraint(a, pltpu.HBM) for a in (
        activations, out_grads, proj_in.T, proj_out.T, doc_ids.reshape(8, 128), doc_order.reshape(8, 128),
        inv_fisher, index_grads)))


def solution(mesh):
    placed = (
        P("idx", "tp"), P("idx", "tp"), P("tp", None), P("tp", None),
        P("idx"), P(), P("tp", None), P(("idx", "tp"), None),
    )
    return jax.shard_map(
        per_device, mesh=mesh, in_specs=placed, out_specs=P(None, ("idx", "tp")), check_vma=False)
```

time: 328 us -> 97.2 us (0.30)
  waiting for transfers between devices: 207 us -> 0 us
  Pallas kernels: 0 us -> 95 us
  blocking collectives: 71 us -> 0 us
  matrix products: 25.2 us -> 0 us
  between operations: 13.5 us -> 0.01 us
  starting transfers between devices: 4.62 us -> 0 us
    all_gather x1 -> x0, waiting for transfers between devices: 198 us -> none  [per_device(): lax.all_gather(queries, ('idx', 'tp'), axis=0, tiled=True)]
    pallas_call x0 -> x1, Pallas kernels: none -> 95 us  [per_device(): pl.pallas_call(kernel, out_shape=pltpu.VMEM((1024, 1024), F32), in_specs=...]
    all_to_all x3 -> x0, blocking collectives: 71 us -> none  [summed_on_arrival(): blocks = lax.all_to_all(cut_along(value, dim, size), axis, 0, 0, tiled=True)]
    dot_general x5 -> x0, matrix products: 25.2 us -> none  [the longest x1 15 us: per_device(): lax.dot_general(lax.all_gather(queries, ('idx', 'tp'), axis=0, tiled=True...]
    all_to_all x1 -> x0, waiting for transfers between devices: 9.71 us -> none  [copy_for_each(): return lax.all_to_all(copies, axis, split_axis=0, concat_axis=0, tiled=True)]
    all_to_all x1 -> x0, starting transfers between devices: 4.59 us -> none  [copy_for_each(): return lax.all_to_all(copies, axis, split_axis=0, concat_axis=0, tiled=True)]
  transfers between devices with their start and end apart: 2 -> 0, of which waited for: 2 -> 0; matrix products, arithmetic and copies ran while one was open for 0% -> 0% of each run, Pallas kernels for 0% -> 0%
where the time goes in v2:
time: 97.2 us; the launch traced here: 97 us
  Pallas kernels  95 us (98%)
  local copies, waits for them, and re-layouts  2.02 us (2%)
    pallas_call x1, Pallas kernels, per_device(): pl.pallas_call(kernel, out_shape=pltpu.VMEM((1024, 1024), F32), in_specs=...  95 us
    unnamed x1, local copies, waits for them, and re-layouts  2.02 us

profile of v2, /device:TPU:1, one launch (start us, length us, event | category | flops | bytes accessed | tf_op | source)
XLA Modules:
  0.0 97.0 jit_solution(14910595169233490169)
XLA Ops:
  0.0 95.0 %influence.1 = f32[1024,1024]{1,0:T(8,128)S(1)} custom-call(bf16[1024,1792]{1,0:T(8,128)(2,1)} %act_hbm.1, bf16[1024,512]{1,0:T(8,128)(2,1)} %og_hbm.1, bf16[64,1792]{1,0:T(8,128)(2,1)} %bitcast.4, bf16[64,512]{1,0:T(8,128)(2,1)} %bitcast.5, s32[8,128]{1,0:T(8,128)} %bitcast.6, s32[8,128]{1,0:T(8,128)} %bitcast.7, f32[256,4096]{1,0:T(8,128)} %f_hbm.1, ...), custom_call_target="tpu_custom_call" | custom-call | tf_op jit(solution)/shard_map/influence/pallas_call | solution.py:522
  95.0 2.0 %copy.10 = f32[1024,1024]{1,0:T(8,128)} copy(f32[1024,1024]{1,0:T(8,128)S(1)} %influence.1) | data formatting | bytes 8388608

commit v3 on v2

--- a/solution.py
+++ b/solution.py
@@ -58,9 +58,9 @@
 
 
 class Gather:
-    def __init__(self, me, bufs, sems):
-        self.me, self.bufs = me, bufs
-        self.out_sem, self.in_sem, self.pass_out, self.pass_in = sems
+    def __init__(self, me, bufs, sems, fine):
+        self.me, self.bufs, self.fine = me, bufs, fine
+        self.out_sem, self.in_sem, self.pass_in = sems
         self.places = {}
         for axis in "xyz":
             for turn in range(2):
@@ -71,9 +71,9 @@
                     self.places[axis, turn, 1, crossed] = base + 1 - 2 * lax.rem(base, 2)
 
     @staticmethod
-    def semaphores():
+    def semaphores(fine):
         dma = pltpu.SemaphoreType.DMA
-        return [dma((COLOURS, 15)), dma((COLOURS, 16)), dma((COLOURS, 8)), dma((COLOURS, 8))]
+        return [dma((COLOURS, 7)), dma((COLOURS, 24 if fine else 16)), dma((COLOURS, 8))]
 
     def at(self, k, subset, octet):
         order = order_of(k)
@@ -107,47 +107,64 @@
             axis, kind = order_of(k)[s]
             move[axis] = self.me.across(axis, kind)
         ref = self.bufs[k].at[(self.me.core, *self.at(k, (), ()))]
-        return self.send(k, ref, n, n, self.me.device(**move))
+        return self.send(k, ref, (0, 2, 1, 1, 3, 3, 3, 3)[n], n, self.me.device(**move))
 
     def onward(self, k, step, octet):
         axis, kind = order_of(k)[step]
         reached = OCTETS.index(octet + (step,))
-        return self.send(k, self.cell_ref(k, self.me.core, octet), 7 + reached, 8 + reached,
+        return self.send(k, self.cell_ref(k, self.me.core, octet), 1 + step, 8 + reached,
                          self.me.next_to(axis, kind))
 
+    def single(self, k, n):
+        ref = self.bufs[k].at[(self.me.core, *self.at(k, SUBSETS[n], ()))]
+        return self.send(k, ref, 4, 16 + n, self.me.next_to(*order_of(k)[3]))
+
     def arrive(self, k, octet):
-        if octet:
-            ref = self.cell_ref(k, self.me.core, octet)
-            self.send(k, ref, 0, 8 + OCTETS.index(octet), self.me.mate()).wait_recv()
+        if octet == (3,) and self.fine:
+            for n in range(8):
+                ref = self.bufs[k].at[(self.me.core, *self.at(k, SUBSETS[n], octet))]
+                self.send(k, ref, 0, 16 + n, self.me.mate()).wait_recv()
             return
-        for n in range(1, 8):
-            ref = self.bufs[k].at[(self.me.core, *self.at(k, SUBSETS[n], ()))]
-            self.send(k, ref, 0, n, self.me.mate()).wait_recv()
+        ref = self.cell_ref(k, self.me.core, octet)
+        self.send(k, ref, 0, 8 + OCTETS.index(octet), self.me.mate()).wait_recv()
 
     def passed(self, k, octet, core):
         n = OCTETS.index(octet)
         ref = self.cell_ref(k, core, octet)
         return pltpu.make_async_remote_copy(
-            src_ref=ref, dst_ref=ref, send_sem=self.pass_out.at[k, n], recv_sem=self.pass_in.at[k, n],
+            src_ref=ref, dst_ref=ref, send_sem=self.out_sem.at[k, 0], recv_sem=self.pass_in.at[k, n],
             device_id=self.me.mate(), device_id_type=MESH)
 
     def start(self):
+        for n in (7, 4, 5, 6, 1, 2, 3):
+            for k in range(COLOURS):
+                self.direct(k, n).start()
+        if self.fine:
+            for k in range(COLOURS):
+                self.single(k, 0).start()
+
+    def forward(self, step, octet):
+        for k in range(COLOURS):
+            self.onward(k, step, octet).start()
+
+    def take(self, octet):
+        step = max((2,) + octet) + 1
         for n in range(1, 8):
             for k in range(COLOURS):
-                self.direct(k, n).start()
-
-    def forward(self, step, octet):
-        for k in range(COLOURS):
-            self.onward(k, step, octet).start()
-
-    def take(self, octet):
-        step = max((2,) + octet) + 1
-        for k in range(COLOURS):
-            self.arrive(k, octet)
-            if step < 6:
+                if octet == ():
+                    ref = self.bufs[k].at[(self.me.core, *self.at(k, SUBSETS[n], ()))]
+                    self.send(k, ref, 0, n, self.me.mate()).wait_recv()
+                    if self.fine:
+                        self.single(k, n).start()
+        if octet == ():
+            if not self.fine:
+                self.forward(3, ())
+            self.forward(4, ())
+        for k in range(COLOURS):
+            if octet:
+                self.arrive(k, octet)
+            if octet and step < 6:
                 self.onward(k, step, octet).start()
-        if octet == ():
-            self.forward(4, ())
         if octet == (3,):
             self.forward(5, ())
             self.forward(5, (3,))
@@ -160,12 +177,11 @@
 
     def close(self):
         for k in range(COLOURS):
-            for n in range(1, 8):
-                self.direct(k, n).wait_send()
-            for octet in OCTETS:
-                for step in range(max((2,) + octet) + 1, 6):
-                    self.onward(k, step, octet).wait_send()
-                self.passed(k, octet, self.me.core).wait_send()
+            whole = self.bufs[k].at[0]
+            for n, ref in enumerate((
+                    whole, whole.at[0, 0, pl.ds(0, 2)], whole.at[0, 0, 0], whole.at[0, 0],
+                    whole.at[0, pl.ds(0, 2)], whole.at[0], whole.at[pl.ds(0, 2)])):
+                self.send(k, ref, n, 0, self.me.mate()).wait_send()
 
 
 def cell_mates(me):
@@ -215,7 +231,7 @@
         starts = []
         for _, z, y, x in spots[0]:
             zn, yn, xn = natural(z, "z"), natural(y, "y"), natural(x, "x")
-            starts.append(pl.multiple_of((lax.rem(zn, 2) * 16 + yn * 4 + xn) * 128, 128))
+            starts.append(pl.multiple_of((zn // 2 * 16 + yn * 4 + xn) * 128, 128))
         lhs = jnp.concatenate([
             jnp.concatenate([bufs[k][s].reshape(rows, 128) for s in blocks], 1) for blocks in spots], 0)
         for tile in range(4):
@@ -226,27 +242,32 @@
                 where = pl.ds(pl.multiple_of(row + FIRST[k] * 16, 16), rows)
                 out_ref[where, cols] += got[n * rows:(n + 1) * rows]
 
-    if "z" in lows:
-        @pl.loop(0, 2)
-        def _(n):
-            z = lows["z"] + n
-            high = natural(z, "z") // 2
-            pairs = [(y, x) for y in spots_of("y") for x in spots_of("x")]
-            for first in range(0, len(pairs), 8):
-                product([[(core, z, y, x) for y, x in pairs[first:first + 8]] for core in range(2)],
-                        [(core * 2 + high) * 256 for core in range(2)])
+    pairs = [(y, x) for y in spots_of("y") for x in spots_of("x")]
+
+    def whole(z_high):
+        for first in range(0, len(pairs), 8):
+            blocks, out_rows = [], []
+            for core in range(2):
+                for z_low in range(2):
+                    z = spot(z_high * 2 + z_low, turned(k, "z"))
+                    blocks.append([(core, z, y, x) for y, x in pairs[first:first + 8]])
+                    out_rows.append((core * 2 + z_low) * 256)
+            product(blocks, out_rows)
+
+    if "z" in lows and not turned(k, "z"):
+        whole(lows["z"] // 2)
         return
 
     @pl.loop(0, 2)
-    def _(z_low):
-        pairs = [(y, x) for y in spots_of("y") for x in spots_of("x")]
-        blocks, out_rows = [], []
-        for core in range(2):
-            for high in range(2):
-                z = spot(high * 2 + z_low, turned(k, "z"))
-                blocks.append([(core, z, y, x) for y, x in pairs])
-                out_rows.append((core * 2 + high) * 256)
-        product(blocks, out_rows)
+    def _(n):
+        if "z" not in lows:
+            whole(n)
+            return
+        z = lows["z"] + n
+        z_low = lax.rem(natural(z, "z"), 2)
+        for first in range(0, len(pairs), 8):
+            product([[(core, z, y, x) for y, x in pairs[first:first + 8]] for core in range(2)],
+                    [(core * 2 + z_low) * 256 for core in range(2)])
 
 
 def kernel(
@@ -270,12 +291,13 @@
     far = [idx_mate(*d) for d in OTHERS_IDX]
 
     loads = [pltpu.make_async_copy(s, d, load_sem.at[n]) for n, (s, d) in enumerate(
-        ((ids_hbm, ids_ref), (order_hbm, order_ref), (pin_hbm, pin), (act_hbm, act), (pout_hbm, pout), (og_hbm, og)))]
+        ((ids_hbm, ids_ref), (order_hbm, order_ref), (pin_hbm, pin), (pout_hbm, pout), (og_hbm, og))
+        + tuple((act_hbm.at[rows], act.at[rows]) for rows in (pl.ds(n * 256, 256) for n in range(4))))]
     for load in loads:
         load.start()
 
     def columns(x, y_low):
-        block = lax.rem(me.z, 2) * 16 + (high * 2 + y_low) * 4 + x
+        block = me.z // 2 * 16 + (high * 2 + y_low) * 4 + x
         return f_hbm.at[:, pl.ds(pl.multiple_of(block * 128, 128), 128)]
 
     own_f = pltpu.make_async_copy(columns(me.x, low), fisher.at[place, core], f_own)
@@ -284,6 +306,44 @@
     barrier = pltpu.get_barrier_semaphore()
     for device in friends:
         pl.semaphore_signal(barrier, inc=1, device_id=device, device_id_type=MESH)
+
+    for load in loads[2:5]:
+        load.wait()
+    def load_g(n):
+        cols = pl.ds(n * 512, 512)
+        return pltpu.make_async_copy(g_hbm.at[:, cols], g_ref.at[n % 2], g_sem.at[n % 2])
+
+    load_g(0).start()
+    load_g(1).start()
+
+    for n in range(4):
+        loads[5 + n].wait()
+        rows = pl.ds(n * 256, 256)
+        both = jnp.concatenate([
+            lax.dot_general(act[rows, :], pin[...], LANES, preferred_element_type=F32),
+            lax.dot_general(og[rows, :], pout[...], LANES, preferred_element_type=F32)], 1)
+        part[pl.ds(n * 2, 2)] = both.reshape(2, 2, 64, 128)
+
+    pl.semaphore_wait(barrier, len(friends))
+
+    f_copies = []
+    for n, d in enumerate(OTHERS_TP):
+        f_copies.append(remote(columns(*tp_mate(*d)), fisher.at[place, core], f_out.at[n], f_in.at[n], others[n]))
+
+    for n in EARLY_F:
+        f_copies[n].start()
+    to_mate = remote(part.at[:, 1 - core], from_mate, mate_sem.at[0], mate_sem.at[1], me.mate())
+    to_mate.start()
+    to_mate.wait()
+    rs_copies = []
+    for q in range(8):
+        mine[q] = part[q, core] + from_mate[q]
+    arrived[p] = mine[p]
+    for n, d in enumerate(OTHERS_TP):
+        x, y = tp_mate(*d)
+        copy = remote(mine.at[y * 4 + x], arrived.at[p], rs_out.at[n], rs_in.at[n], others[n])
+        copy.start()
+        rs_copies.append(copy)
 
     loads[0].wait()
     loads[1].wait()
@@ -300,59 +360,13 @@
     for r in range(8):
         counts_ref[r:r + 1, :] = jnp.sum(less[r], 0, keepdims=True)
         counts_ref[8 + r:9 + r, :] = jnp.sum(same_doc[r], 0, keepdims=True)
-    for load in loads[2:]:
-        load.wait()
-    def load_g(n):
-        cols = pl.ds(n * 512, 512)
-        return pltpu.make_async_copy(g_hbm.at[:, cols], g_ref.at[n % 2], g_sem.at[n % 2])
-
-    load_g(0).start()
-    load_g(1).start()
-
-    @pl.loop(0, 4)
-    def _(n):
-        rows = pl.ds(pl.multiple_of(n * 256, 256), 256)
-        both = jnp.concatenate([
-            lax.dot_general(act[rows, :], pin[...], LANES, preferred_element_type=F32),
-            lax.dot_general(og[rows, :], pout[...], LANES, preferred_element_type=F32)], 1)
-        part[pl.ds(n * 2, 2)] = both.reshape(2, 2, 64, 128)
-
-    pl.semaphore_wait(barrier, len(friends))
-
     shard = lax.axis_index("idx")
     count_copies = []
     for n, device in enumerate(far):
         copy = remote(counts_ref, their_counts.at[shard], c_out.at[n], c_in.at[n], device)
         copy.start()
         count_copies.append(copy)
-    f_copies = []
-    for n, d in enumerate(OTHERS_TP):
-        f_copies.append(remote(columns(*tp_mate(*d)), fisher.at[place, core], f_out.at[n], f_in.at[n], others[n]))
-
-    to_mate = remote(part.at[:, 1 - core], from_mate, mate_sem.at[0], mate_sem.at[1], me.mate())
-    to_mate.start()
-    to_mate.wait()
-    rs_copies = []
-    for q in range(8):
-        mine[q] = part[q, core] + from_mate[q]
-    arrived[p] = mine[p]
-    for n, d in enumerate(OTHERS_TP):
-        x, y = tp_mate(*d)
-        copy = remote(mine.at[y * 4 + x], arrived.at[p], rs_out.at[n], rs_in.at[n], others[n])
-        copy.start()
-        rs_copies.append(copy)
-
     their_counts[shard] = counts_ref[...]
-    for copy in count_copies:
-        copy.wait_recv()
-    summed = their_counts[0]
-    for n in range(1, 8):
-        summed = summed + their_counts[n]
-    counts_sum[...] = summed
-    to_scalar = pltpu.make_async_copy(counts_sum, counts, c_sem)
-    to_scalar.start()
-    to_scalar.wait()
-
 
     def turn(*chunks):
         for n in chunks:
@@ -372,13 +386,13 @@
     total = arrived[0]
     for q in range(1, 8):
         total = total + arrived[q]
-    gather = Gather(me, bufs, sems[:4])
+    gather = Gather(me, bufs, sems[:3], False)
     for k in range(COLOURS):
         own = gather.at(k, (), ())
         row = T_FIRST[k] * 8
         bufs[k][(core, *own)] = total[row:row + T_UNITS[k] * 8].reshape(T_UNITS[k], 8, 128)
     gather.start()
-    for n in EARLY_F:
+    for n in LATE_F:
         f_copies[n].start()
     turn(2, 3, 4)
 
@@ -404,15 +418,22 @@
             gather.from_mate(OCTETS[n - 1])
             spread(OCTETS[n - 1])
         if n == 1:
-            for m in LATE_F:
-                f_copies[m].start()
+            for copy in count_copies:
+                copy.wait_recv()
+            summed = their_counts[0]
+            for n in range(1, 8):
+                summed = summed + their_counts[n]
+            counts_sum[...] = summed
+            to_scalar = pltpu.make_async_copy(counts_sum, counts, c_sem)
+            to_scalar.start()
         if n == 3:
             for m in LAST_F:
                 f_copies[m].start()
     gather.from_mate(OCTETS[7])
     spread(OCTETS[7])
 
-    first_row = (core * 2 + me.z // 2) * 256
+    to_scalar.wait()
+    first_row = (core * 2 + lax.rem(me.z, 2)) * 256
     lane = lax.broadcasted_iota(jnp.int32, (128, 128), 1)
     sub = lax.broadcasted_iota(jnp.int32, (32, 128), 0)
     same = lax.broadcasted_iota(jnp.int32, (128, 256), 0) // 32 == lax.rem(
@@ -466,31 +487,35 @@
         lacc[...] += jnp.dot(d_low, f_high, preferred_element_type=F32)
 
     block = (acc[:, :128] + acc[:, 128:] + lacc[...]).astype(BF16)
-    scores = Gather(me, qbufs, sems[4:])
+    scores = Gather(me, qbufs, sems[3:], True)
     for k in range(COLOURS):
         first = FIRST[k] * 16
         qbufs[k][(core, *scores.at(k, (), ()))] = block[first:first + UNITS[k] * 16].reshape(UNITS[k], 16, 128)
     scores.start()
     out_ref[...] = jnp.zeros_like(out_ref)
-    for octet in OCTETS[:4]:
-        scores.take(octet)
-    for octet in OCTETS[:4]:
-        scores.from_mate(octet)
-    for n, octet in enumerate(OCTETS[4:]):
-        for k in range(2 * n, min(2 * n + 2, COLOURS)):
-            multiply(scores, k, {5: 0}, qbufs, gt_ref, out_ref)
-        if n < 3:
-            scores.take(octet)
-    for octet in OCTETS[4:6]:
-        scores.from_mate(octet)
+    scores.take(OCTETS[0])
+    scores.from_mate(OCTETS[0])
     for k in range(COLOURS):
-        multiply(scores, k, {4: 0, 5: 1}, qbufs, gt_ref, out_ref)
-        if k == 3:
-            scores.take(OCTETS[7])
-    for octet in OCTETS[6:]:
-        scores.from_mate(octet)
-    for k in range(COLOURS):
-        multiply(scores, k, {4: 1, 5: 1}, qbufs, gt_ref, out_ref)
+        multiply(scores, k, {3: 0, 4: 0, 5: 0}, qbufs, gt_ref, out_ref)
+    scores.take(OCTETS[1])
+    scores.from_mate(OCTETS[1])
+
+    def part_scores(crossed, meanwhile):
+        for k in range(COLOURS):
+            multiply(scores, k, crossed, qbufs, gt_ref, out_ref)
+            if k in meanwhile:
+                scores.take(OCTETS[meanwhile[k]])
+
+    part_scores({3: 1, 4: 0, 5: 0}, {2: 2, 5: 3})
+    scores.from_mate(OCTETS[2])
+    scores.from_mate(OCTETS[3])
+    part_scores({4: 1, 5: 0}, {1: 4, 4: 5})
+    scores.from_mate(OCTETS[4])
+    scores.from_mate(OCTETS[5])
+    part_scores({4: 0, 5: 1}, {1: 6, 4: 7})
+    scores.from_mate(OCTETS[6])
+    scores.from_mate(OCTETS[7])
+    part_scores({4: 1, 5: 1}, {})
 
     for copy in count_copies + f_copies + rs_copies + [pass_f]:
         copy.wait_send()
@@ -517,14 +542,14 @@
                 pltpu.VMEM((32 * PITCH, 128), F32), pltpu.VMEM((256, 256), F32), pltpu.VMEM((256, 128), F32)]
     scratch += [pltpu.VMEM((2, 4, 4, 4, n, 16, 128), BF16) for n in UNITS]
     scratch += [pltpu.VMEM((2, 1024, 512), BF16), pltpu.VMEM((4096, 1024), BF16)]
-    scratch += [dma((6,)), dma((2,)), dma((7,)), dma((7,)), dma((7,)), dma((7,)), dma((2,)), dma, dma((7,)), dma((7,)),
+    scratch += [dma((9,)), dma((2,)), dma((7,)), dma((7,)), dma((7,)), dma((7,)), dma((2,)), dma, dma((7,)), dma((7,)),
                 dma, dma((2,))]
     return pl.pallas_call(
         kernel,
         out_shape=pltpu.VMEM((1024, 1024), F32),
         in_specs=[hbm] * 8,
         out_specs=vmem,
-        scratch_shapes=scratch + Gather.semaphores() + Gather.semaphores(),
+        scratch_shapes=scratch + Gather.semaphores(False) + Gather.semaphores(True),
         compiler_params=pltpu.CompilerParams(collective_id=2, has_side_effects=True, vmem_limit_bytes=46 << 20),
         name="influence",
     )(*(pltpu.with_memory_space_constraint(a, pltpu.HBM) for a in (

time: 97.2 us -> 91.3 us (0.939)
  Pallas kernels: 95 us -> 89.1 us
    pallas_call x1, Pallas kernels: 95 us -> 89.1 us  [per_device(): pl.pallas_call(kernel, out_shape=pltpu.VMEM((1024, 1024), F32), in_specs=...]
where the time goes in v3:
time: 91.3 us; the launch traced here: 91.2 us
  Pallas kernels  89.1 us (98%)
  local copies, waits for them, and re-layouts  2.02 us (2%)
    pallas_call x1, Pallas kernels, per_device(): pl.pallas_call(kernel, out_shape=pltpu.VMEM((1024, 1024), F32), in_specs=...  89.1 us
    unnamed x1, local copies, waits for them, and re-layouts  2.02 us

profile of v3, /device:TPU:1, one launch (start us, length us, event | category | flops | bytes accessed | tf_op | source)
XLA Modules:
  0.0 91.2 jit_solution(3734577626727791634)
XLA Ops:
  0.0 89.1 %influence.1 = f32[1024,1024]{1,0:T(8,128)S(1)} custom-call(bf16[1024,1792]{1,0:T(8,128)(2,1)} %act_hbm.1, bf16[1024,512]{1,0:T(8,128)(2,1)} %og_hbm.1, bf16[64,1792]{1,0:T(8,128)(2,1)} %bitcast.4, bf16[64,512]{1,0:T(8,128)(2,1)} %bitcast.5, s32[8,128]{1,0:T(8,128)} %bitcast.6, s32[8,128]{1,0:T(8,128)} %bitcast.7, f32[256,4096]{1,0:T(8,128)} %f_hbm.1, ...), custom_call_target="tpu_custom_call" | custom-call | tf_op jit(solution)/shard_map/influence/pallas_call | solution.py:547
  89.1 2.0 %copy.10 = f32[1024,1024]{1,0:T(8,128)} copy(f32[1024,1024]{1,0:T(8,128)S(1)} %influence.1) | data formatting | bytes 8388608
